TPU v7x, 32 devices: a whole 2x2x4 slice. The times are simulated.
32 devices in a mesh: groups: 2 (over y), band: 4 (over z), chan: 4 (over x, core).
Axes of the slice: x: 2, y: 2, z: 4, core: 2. Of those that a mesh axis runs over, the one named last changes fastest.
Arguments:
- slide_region: float32 [16, 32, 8192], P('chan', ('groups', 'band')), parts along dimension 1, may hold values from -6 to 6
- row_taps: float32 [16, 257], P('chan'), may hold values from -0.375 to 0.375
- column_taps: float32 [16, 257], replicated, may hold values from -0.375 to 0.375
- channel_mix: float32 [16, 16], replicated, may hold values from -1.5 to 1.5
Outputs:
- filtered: float32 [16, 32, 8192], P('chan', ('groups', 'band')), parts along dimension 1
There are 2 independent parts, one for each index of `groups`. A program takes and returns all parts, laid end to end along the dimension named above; an argument that names none is the same for every part. Nothing has to cross between parts.
All inputs are finite; a program needn't handle non-finite values.
Results may differ from a plain program's by a relative error of at most 0.00007.
Values sent between devices are 32-bit elements; how exact they have to be, the bound alone decides.
A program may use at most 64 MiB of HBM per device.

v0:
```python
import jax
import jax.numpy as jnp
from jax import lax
from jax.sharding import PartitionSpec as P

precise = lax.Precision.HIGHEST


def band_tables(filter_taps, tile_size):
    channels, length = filter_taps.shape
    margin = (length - 1) // 2
    period = 4 * tile_size
    border = 3 * tile_size + length
    widened = jnp.pad(filter_taps, ((0, 0), (border, border)))
    lowest = margin - tile_size + border
    window = widened[:, lowest : lowest + 3 * tile_size]
    vector = jnp.pad(window, ((0, 0), (0, tile_size)))
    repeated = jnp.tile(vector, (1, tile_size))[:, : tile_size * (period - 1)]
    toeplitz = repeated.reshape(channels, tile_size, period - 1)[:, :, : 3 * tile_size]
    stacked = jnp.transpose(toeplitz, (0, 2, 1))
    return stacked.reshape(channels, 3, tile_size, tile_size)


def along_columns(signal, filter_taps):
    tile_size = 128
    tables = band_tables(filter_taps, tile_size)
    channels, row_count, col_count = signal.shape
    tile_count = col_count // tile_size
    tiled = signal.reshape(channels, row_count, tile_count, tile_size)
    padded = jnp.pad(tiled, ((0, 0), (0, 0), (1, 1), (0, 0)))
    result = jnp.einsum(
        "crti,cij->crtj", padded[:, :, 0:tile_count], tables[:, 0], precision=precise
    )
    result = result + jnp.einsum(
        "crti,cij->crtj", padded[:, :, 1 : tile_count + 1], tables[:, 1], precision=precise
    )
    result = result + jnp.einsum(
        "crti,cij->crtj", padded[:, :, 2:], tables[:, 2], precision=precise
    )
    return result.reshape(channels, row_count, col_count)


def along_rows(signal, filter_taps):
    channels, row_count, col_count = signal.shape
    tile_size = 128 if row_count % 128 == 0 else row_count
    tables = band_tables(filter_taps, tile_size)
    tile_count = row_count // tile_size
    tiled = signal.reshape(channels, tile_count, tile_size, col_count)
    padded = jnp.pad(tiled, ((0, 0), (1, 1), (0, 0), (0, 0)))
    result = jnp.einsum("ctiw,cij->ctjw", padded[:, 0:tile_count], tables[:, 0], precision=precise)
    result = result + jnp.einsum(
        "ctiw,cij->ctjw", padded[:, 1 : tile_count + 1], tables[:, 1], precision=precise
    )
    result = result + jnp.einsum("ctiw,cij->ctjw", padded[:, 2:], tables[:, 2], precision=precise)
    return result.reshape(channels, row_count, col_count)


def on_device(slide_region, row_taps, column_taps, channel_mix):
    local_channels = slide_region.shape[0]
    across = along_columns(slide_region, row_taps)
    column_band = lax.all_to_all(across, "band", split_axis=2, concat_axis=1, tiled=True)
    first_channel = lax.axis_index("chan") * local_channels
    own_taps = lax.dynamic_slice_in_dim(column_taps, first_channel, local_channels, 0)
    vertical = along_rows(column_band, own_taps)
    own_mixing = lax.dynamic_slice_in_dim(channel_mix, first_channel, local_channels, 0)
    blended = jnp.einsum(
        "oc,chw->ohw",
        own_mixing,
        lax.all_gather(vertical, "chan", axis=0, tiled=True),
        precision=precise,
    )
    return lax.all_to_all(blended, "band", split_axis=1, concat_axis=2, tiled=True)


def solution(mesh):
    in_specs = (P("chan", ("groups", "band"), None), P("chan", None), P(), P())
    out_specs = P("chan", ("groups", "band"), None)
    return jax.shard_map(
        on_device, mesh=mesh, in_specs=in_specs, out_specs=out_specs, check_vma=False
    )
```

profile of v0, /device:TPU:0, one launch (start us, length us, event | category | flops | bytes accessed | tf_op | source)
XLA Modules:
  0.0 165.2 jit_solution(12233661536541176305)
XLA Ops:
  6.5 0.7 pad_slice_fusion.4
  7.4 0.7 copy.47
  8.2 1.0 reshape.47
  9.5 0.4 reshape.46
  9.9 0.6 fusion.4
  10.5 0.6 fusion.5
  11.2 0.6 fusion.3
  11.8 8.6 %copy.38 = f32[4,4,64,128]{1,0,3,2:T(4,128)} copy(f32[4,4,64,128]{3,2,1,0:T(8,128)S(1)} %fusion.3) | data formatting | bytes 1048576 | tf_op jit(solution)/shard_map/reshape | solution.py:40
  20.4 24.6 %reshape.55 = f32[4,1,32768]{2,1,0:T(1,128)} reshape(f32[8192,4,4]{2,1,0:T(4,128)} %bitcast.68) | data formatting | bytes 1048576
  45.0 6.3 %all-to-all-start = ((f32[4,1,32768]{2,1,0:T(1,128)}), f32[4,1,32768]{2,1,0:T(1,128)S(1)}, u32[]{:S(2)}, u32[]{:S(2)}) async-start(f32[4,1,32768]{2,1,0:T(1,128)} %reshape.55), calls=%async_computation | async-start | bytes 1048576 | tf_op jit(solution)/shard_map/all_to_all | solution.py:61
  51.3 0.8 dynamic-slice
  52.5 0.4 fusion.8
  52.9 13.0 %all-to-all-done = f32[4,1,32768]{2,1,0:T(1,128)S(1)} async-done(((f32[4,1,32768]{2,1,0:T(1,128)}), f32[4,1,32768]{2,1,0:T(1,128)S(1)}, u32[]{:S(2)}, u32[]{:S(2)}) %all-to-all-start) | async-done | bytes 524320 | tf_op jit(solution)/shard_map/all_to_all | solution.py:61
  65.8 0.5 broadcast.18
  66.3 2.2 %reduce = f32[4,32768]{1,0:T(4,128)S(1)} reduce(f32[4,1,32768]{2,1,0:T(1,128)S(1)} %all-to-all-done, f32[]{:T(128)} %broadcast.18), dimensions={1}, to_apply=%all_to_all.24.reduce_sub_computation | reduce | bytes 1048580 | tf_op jit(solution)/shard_map/all_to_all | solution.py:61
  68.5 28.0 %reshape.56 = f32[8192,4,4]{2,1,0:T(4,128)} reshape(f32[4,32768]{1,0:T(4,128)S(1)} %reduce) | data formatting | bytes 1048576
  96.5 13.4 %copy.30 = f32[4,4,4,2048]{3,0,2,1:T(4,128)S(1)} copy(f32[4,4,4,2048]{2,0,3,1:T(4,128)} %bitcast.69) | data formatting | bytes 1048576 | tf_op jit(solution)/shard_map/all_to_all | solution.py:61
  109.9 0.9 convolution_add_fusion.1
  110.8 1.1 convolution_add_fusion
  111.9 21.8 %all-gather.2.cloned.1.call-done = f32[16,16,2048]{2,1,0:T(8,128)} async-done(((f32[4,16,2048]{2,1,0:T(8,128)}), f32[16,16,2048]{2,1,0:T(8,128)}) %all-gather.2.cloned.1.call-update) | async-done | bytes 2097168 | tf_op jit(solution)/shard_map/all_gather | solution.py:69
  133.8 3.8 %fusion = f32[4,16,2048]{2,0,1:T(4,128)S(1)} fusion(f32[16,16,2048]{2,1,0:T(8,128)} %all-gather.2.cloned.1.call-done, f32[16,16]{1,0:T(8,128)S(1)} %copy-done, s32[]{:T(128)S(6)} %select_n.4), kind=kOutput, calls=%fused_computation.2 | convolution fusion | flops 25165824 | bytes 2623492 | tf_op jit(solution)/shard_map/oc,chw->ohw/dot_general | solution.py:66
  137.5 19.3 %all_to_all.33 = f32[4,16,2048]{2,0,1:T(4,128)S(1)} all-to-all(f32[4,16,2048]{2,0,1:T(4,128)S(1)} %fusion), channel_id=1, replica_groups=mesh['groups'=2,'band'=4,'chan'=4] {'band'}, dimensions={1} | all-to-all | bytes 1048576 | tf_op jit(solution)/shard_map/all_to_all | solution.py:72
  156.8 0.3 copy.34
  157.2 1.2 all_to_all.30
  (18 shorter events, 0.9 us)
Async XLA Ops:
  6.5 127.2 %copy-start = (f32[16,16]{1,0:T(8,128)S(1)}, f32[16,16]{1,0:T(8,128)}, u32[]{:S(2)}) copy-start(f32[16,16]{1,0:T(8,128)} %param.7) | copy-start | bytes 3076
  8.1 1.4 copy-start.1
  45.0 20.8 %all-to-all-start = ((f32[4,1,32768]{2,1,0:T(1,128)}), f32[4,1,32768]{2,1,0:T(1,128)S(1)}, u32[]{:S(2)}, u32[]{:S(2)}) async-start(f32[4,1,32768]{2,1,0:T(1,128)} %reshape.55), calls=%async_computation | async-start | bytes 1048576 | tf_op jit(solution)/shard_map/all_to_all | solution.py:61
  51.3 82.4 %all-gather.2.cloned.1.call-start = ((), (), s32[]{:S(2)}) async-start(), calls=%async_computation.2 | async-start | bytes 2621440 | tf_op jit(solution)/shard_map/all_gather | solution.py:69
Sparse Core Ops, SparseCore 0:
  112.1 21.6 all-gather.1
where the time goes:
time: 166 us; the launch traced here: 165 us
  local copies, waits for them, and re-layouts  81.1 us (49%)
  waiting for transfers between devices  34.8 us (21%)
  blocking collectives  19.3 us (12%)
  between operations  13.5 us (8%)
  matrix products  7.99 us (5%)
  starting transfers between devices  6.35 us (4%)
  other arithmetic  2.17 us (1%)
    unnamed x8, local copies, waits for them, and re-layouts  53.4 us
    all_gather x1, waiting for transfers between devices, on_device(): lax.all_gather(vertical, 'chan', axis=0, tiled=True)  21.8 us
    all_to_all x1, blocking collectives, on_device(): lax.all_to_all(blended, 'band', split_axis=1, concat_axis=2, tiled=True)  19.3 us
    all_to_all x2, local copies, waits for them, and re-layouts, on_device(): lax.all_to_all(across, 'band', split_axis=2, concat_axis=1, tiled=True)  13.9 us
    all_to_all x1, waiting for transfers between devices, on_device(): lax.all_to_all(across, 'band', split_axis=2, concat_axis=1, tiled=True)  13 us
    reshape x1, local copies, waits for them, and re-layouts, along_columns(): return result.reshape(channels, row_count, col_count)  8.62 us
    all_to_all x1, starting transfers between devices, on_device(): lax.all_to_all(across, 'band', split_axis=2, concat_axis=1, tiled=True)  6.35 us
    dot_general x1, matrix products, on_device(): jnp.einsum('oc,chw->ohw', own_mixing, lax.all_gather(vertical, 'chan', ax...  3.77 us
  transfers between devices with their start and end apart: 2, of which 2 were waited for; matrix products, arithmetic and copies ran while one was open for 1% of the time, Pallas kernels for 0%

commit v1 on v0

--- a/solution.py
+++ b/solution.py
@@ -63,12 +63,22 @@
     own_taps = lax.dynamic_slice_in_dim(column_taps, first_channel, local_channels, 0)
     vertical = along_rows(column_band, own_taps)
     own_mixing = lax.dynamic_slice_in_dim(channel_mix, first_channel, local_channels, 0)
-    blended = jnp.einsum(
-        "oc,chw->ohw",
-        own_mixing,
-        lax.all_gather(vertical, "chan", axis=0, tiled=True),
-        precision=precise,
-    )
+    size, here, rows = (lax.axis_size("chan"), lax.axis_index("chan"), vertical.shape[0])
+    forward = [(i, (i + 1) % size) for i in range(size)]
+    block, total = (vertical, None)
+    for hop in range(size):
+        arriving = lax.ppermute(block, "chan", forward) if hop < size - 1 else None
+        update = jnp.einsum(
+            "oc,chw->ohw",
+            lax.dynamic_slice_in_dim(
+                own_mixing, (here - hop) % size * rows, block.shape[0], axis=1
+            ),
+            block,
+            precision=precise,
+        )
+        total = update if total is None else total + update
+        block = arriving
+    blended = total
     return lax.all_to_all(blended, "band", split_axis=1, concat_axis=2, tiled=True)
 
 

time: 166 us -> 151 us (0.910)
  between operations: 13.5 us -> 0.18 us
  blocking collectives: 19.3 us -> 16.5 us
    ppermute x0 -> x3, waiting for transfers between devices: none -> 21.9 us  [on_device(): arriving = lax.ppermute(block, 'chan', forward) if hop < size - 1 else None]
    all_gather x1 -> x0, waiting for transfers between devices: 21.8 us -> none  [on_device(): lax.all_gather(vertical, 'chan', axis=0, tiled=True)]
    all_to_all x1, blocking collectives: 19.3 us -> 16.5 us  [on_device(): lax.all_to_all(blended, 'band', split_axis=1, concat_axis=2, tiled=True)]
    dot_general x1 -> x4, matrix products: 3.77 us -> 5.18 us  [on_device(): jnp.einsum('oc,chw->ohw', lax.dynamic_slice_in_dim(own_mixing, (here - ho...]
    unnamed x8 -> x6, local copies, waits for them, and re-layouts: 53.4 us -> 53.4 us
  transfers between devices with their start and end apart: 2 -> 4, of which waited for: 2 -> 4; matrix products, arithmetic and copies ran while one was open for 1% -> 4% of each run, Pallas kernels for 0% -> 0%
where the time goes in v1:
time: 151 us
  local copies, waits for them, and re-layouts  82.3 us (55%)
  waiting for transfers between devices  34.9 us (23%)
  blocking collectives  16.5 us (11%)
  matrix products  8.32 us (6%)
  starting transfers between devices  6.41 us (4%)
  other arithmetic  2.17 us (1%)
    unnamed x6, local copies, waits for them, and re-layouts  53.4 us
    ppermute x3, waiting for transfers between devices, on_device(): arriving = lax.ppermute(block, 'chan', forward) if hop < size - 1 else None  21.9 us
    all_to_all x1, blocking collectives, on_device(): lax.all_to_all(blended, 'band', split_axis=1, concat_axis=2, tiled=True)  16.5 us
    all_to_all x2, local copies, waits for them, and re-layouts, on_device(): lax.all_to_all(across, 'band', split_axis=2, concat_axis=1, tiled=True)  13.9 us
    all_to_all x1, waiting for transfers between devices, on_device(): lax.all_to_all(across, 'band', split_axis=2, concat_axis=1, tiled=True)  12.9 us
    reshape x1, local copies, waits for them, and re-layouts, along_columns(): return result.reshape(channels, row_count, col_count)  8.59 us
    all_to_all x1, starting transfers between devices, on_device(): lax.all_to_all(across, 'band', split_axis=2, concat_axis=1, tiled=True)  6.35 us
    dot_general x4, matrix products, on_device(): jnp.einsum('oc,chw->ohw', lax.dynamic_slice_in_dim(own_mixing, (here - ho...  5.18 us
  transfers between devices with their start and end apart: 4, of which 4 were waited for; matrix products, arithmetic and copies ran while one was open for 4% of the time, Pallas kernels for 0%

profile of v1, /device:TPU:0, one launch (start us, length us, event | category | flops | bytes accessed | tf_op | source)
XLA Modules:
  0.0 150.7 jit_solution(8703117496081549901)
XLA Ops:
  0.0 1.4 reshape.46
  1.4 0.7 pad_slice_fusion.4
  2.3 0.7 copy.48
  3.0 1.0 reshape.47
  4.4 0.6 fusion.3
  5.0 0.6 fusion.2
  5.6 0.6 fusion.1
  6.3 8.6 %copy.41 = f32[4,4,64,128]{1,0,3,2:T(4,128)} copy(f32[4,4,64,128]{3,2,1,0:T(8,128)S(1)} %fusion.1) | data formatting | bytes 1048576 | tf_op jit(solution)/shard_map/reshape | solution.py:40
  14.8 24.6 %reshape.58 = f32[4,1,32768]{2,1,0:T(1,128)} reshape(f32[8192,4,4]{2,1,0:T(4,128)} %bitcast.75) | data formatting | bytes 1048576
  39.4 6.4 %all-to-all-start = ((f32[4,1,32768]{2,1,0:T(1,128)}), f32[4,1,32768]{2,1,0:T(1,128)S(1)}, u32[]{:S(2)}, u32[]{:S(2)}) async-start(f32[4,1,32768]{2,1,0:T(1,128)} %reshape.58), calls=%async_computation | async-start | bytes 1048576 | tf_op jit(solution)/shard_map/all_to_all | solution.py:61
  45.8 0.8 dynamic-slice
  47.3 12.9 %all-to-all-done = f32[4,1,32768]{2,1,0:T(1,128)S(1)} async-done(((f32[4,1,32768]{2,1,0:T(1,128)}), f32[4,1,32768]{2,1,0:T(1,128)S(1)}, u32[]{:S(2)}, u32[]{:S(2)}) %all-to-all-start) | async-done | bytes 524320 | tf_op jit(solution)/shard_map/all_to_all | solution.py:61
  60.8 2.2 %reduce = f32[4,32768]{1,0:T(4,128)S(1)} reduce(f32[4,1,32768]{2,1,0:T(1,128)S(1)} %all-to-all-done, f32[]{:T(128)} %broadcast.22), dimensions={1}, to_apply=%all_to_all.24.reduce_sub_computation | reduce | bytes 1048580 | tf_op jit(solution)/shard_map/all_to_all | solution.py:61
  63.0 28.0 %reshape.59 = f32[8192,4,4]{2,1,0:T(4,128)} reshape(f32[4,32768]{1,0:T(4,128)S(1)} %reduce) | data formatting | bytes 1048576
  91.0 13.4 %copy.31 = f32[4,4,4,2048]{3,1,2,0:T(4,128)S(1)} copy(f32[4,4,4,2048]{1,0,3,2:T(4,128)} %bitcast.76) | data formatting | bytes 1048576 | tf_op jit(solution)/shard_map/all_to_all | solution.py:61
  105.6 8.6 %collective-permute-done = f32[4,16,2048]{2,1,0:T(8,128)S(1)} collective-permute-done((f32[4,16,2048]{2,1,0:T(8,128)S(1)}, f32[4,16,2048]{2,1,0:T(8,128)S(1)}, u32[]{:S(2)}, u32[]{:S(2)}) %collective-permute-start) | collective-permute-done | bytes 524320 | tf_op jit(solution)/shard_map/ppermute | solution.py:70
  114.2 1.3 fusion.7
  115.4 7.3 %collective-permute-done.1 = f32[4,16,2048]{2,1,0:T(8,128)S(1)} collective-permute-done((f32[4,16,2048]{2,1,0:T(8,128)S(1)}, f32[4,16,2048]{2,1,0:T(8,128)S(1)}, u32[]{:S(2)}, u32[]{:S(2)}) %collective-permute-start.1) | collective-permute-done | bytes 524320 | tf_op jit(solution)/shard_map/ppermute | solution.py:70
  122.8 1.3 convolution_add_fusion.2
  124.1 1.3 convolution_add_fusion.1
  125.4 6.0 %collective-permute-done.2 = f32[4,16,2048]{2,1,0:T(8,128)S(1)} collective-permute-done((f32[4,16,2048]{2,1,0:T(8,128)S(1)}, f32[4,16,2048]{2,1,0:T(8,128)S(1)}, u32[]{:S(2)}, u32[]{:S(2)}) %collective-permute-start.2) | collective-permute-done | bytes 524320 | tf_op jit(solution)/shard_map/ppermute | solution.py:70
  131.4 1.3 convolution_add_fusion
  132.7 16.5 %all_to_all.33 = f32[4,16,2048]{2,0,1:T(4,128)S(1)} all-to-all(f32[4,16,2048]{2,0,1:T(4,128)S(1)} %convolution_add_fusion), channel_id=1, replica_groups=mesh['groups'=2,'band'=4,'chan'=4] {'band'}, dimensions={1} | all-to-all | bytes 1048576 | tf_op jit(solution)/shard_map/all_to_all | solution.py:82
  149.5 1.2 all_to_all.30
  (23 shorter events, 3.3 us)
Async XLA Ops:
  0.0 114.2 %copy-start = (f32[16,16]{1,0:T(8,128)S(1)}, f32[16,16]{1,0:T(8,128)}, u32[]{:S(2)}) copy-start(f32[16,16]{1,0:T(8,128)} %param.7) | copy-start | bytes 3076
  39.4 20.8 %all-to-all-start = ((f32[4,1,32768]{2,1,0:T(1,128)}), f32[4,1,32768]{2,1,0:T(1,128)S(1)}, u32[]{:S(2)}, u32[]{:S(2)}) async-start(f32[4,1,32768]{2,1,0:T(1,128)} %reshape.58), calls=%async_computation | async-start | bytes 1048576 | tf_op jit(solution)/shard_map/all_to_all | solution.py:61
  105.5 8.7 %collective-permute-start = (f32[4,16,2048]{2,1,0:T(8,128)S(1)}, f32[4,16,2048]{2,1,0:T(8,128)S(1)}, u32[]{:S(2)}, u32[]{:S(2)}) collective-permute-start(f32[4,16,2048]{2,1,0:T(8,128)S(1)} %convolution_add_fusion.3), channel_id=1, source_target_pairs={{0,1},{1,2},{2,3},{3,0},{4,5},{5,6},{6,7},{7,4},{8,9},{9,10},{10,1... | collective-permute-start | bytes 1572872 | tf_op jit(solution)/shard_map/ppermute | solution.py:70
  114.2 8.6 %collective-permute-start.1 = (f32[4,16,2048]{2,1,0:T(8,128)S(1)}, f32[4,16,2048]{2,1,0:T(8,128)S(1)}, u32[]{:S(2)}, u32[]{:S(2)}) collective-permute-start(f32[4,16,2048]{2,1,0:T(8,128)S(1)} %collective-permute-done), channel_id=1, source_target_pairs={{0,1},{1,2},{2,3},{3,0},{4,5},{5,6},{6,7},{7,4},{8,9},{9,10},{10,1... | collective-permute-start | bytes 1572872 | tf_op jit(solution)/shard_map/ppermute | solution.py:70
  122.8 8.6 %collective-permute-start.2 = (f32[4,16,2048]{2,1,0:T(8,128)S(1)}, f32[4,16,2048]{2,1,0:T(8,128)S(1)}, u32[]{:S(2)}, u32[]{:S(2)}) collective-permute-start(f32[4,16,2048]{2,1,0:T(8,128)S(1)} %collective-permute-done.1), channel_id=1, source_target_pairs={{0,1},{1,2},{2,3},{3,0},{4,5},{5,6},{6,7},{7,4},{8,9},{9,10},{10,1... | collective-permute-start | bytes 1572872 | tf_op jit(solution)/shard_map/ppermute | solution.py:70
